TPU v7x, 32 devices: a whole 2x2x4 slice. The times are simulated.
32 devices in a mesh: group: 1, pool: 1, slab: 32 (over z, y, x, core).
Axes of the slice: x: 2, y: 2, z: 4, core: 2. Of those that a mesh axis runs over, the one named last changes fastest.
Arguments:
- drho_part: float32 [1, 16, 2, 128, 128, 128], P('pool', 'group', None, 'slab'), may hold values from -6 to 6
- fxc: float32 [128, 128, 128], P('slab'), may hold values from -2 to -0.2
- cutoff_mask: int32 [128, 128, 128], P(None, 'slab'), may hold values 0 or 1
- owner_table: int32 [16], P('group'), may hold values from 0 to 15, each once
Outputs:
- dv: float32 [16, 2, 128, 128, 128], P('group', None, 'slab')
Inputs may be any that keep to these rules, and one draw needn't show every extreme that they name: `owner_table`: each perturbation appears in exactly one slot.
All inputs are finite; a program needn't handle non-finite values. No bound on the sum of `cutoff_mask` on one device may be relied on, other than what follows from the above.
Results may differ from a plain program's by a relative error of at most 0.00008.
Values sent between devices are 32-bit elements; how exact they have to be, the bound alone decides.
A program may use at most 128 MiB of HBM per device.

v0:
```python
import math

import jax
import jax.numpy as jnp
from jax import lax
from jax.sharding import PartitionSpec as P


def dft_tables(length):
    index = jnp.arange(length, dtype=jnp.int32)
    phase = index[:, None] * index[None, :] % length
    angle = phase.astype(jnp.float32) * (2.0 * math.pi / length)
    return (jnp.cos(angle), jnp.sin(angle))


def transform(field, form, cosine, sine, orient):
    real_part = field[:, 0]
    imag_part = field[:, 1]
    highest = lax.Precision.HIGHEST
    real_cos = jnp.einsum(form, real_part, cosine, precision=highest)
    real_sin = jnp.einsum(form, real_part, sine, precision=highest)
    imag_cos = jnp.einsum(form, imag_part, cosine, precision=highest)
    imag_sin = jnp.einsum(form, imag_part, sine, precision=highest)
    return jnp.stack([real_cos - orient * imag_sin, imag_cos + orient * real_sin], axis=1)


def frequency(index, length):
    return ((index + length // 2) % length - length // 2).astype(jnp.float32)


def column_kernel(cutoff_mask, length):
    width = cutoff_mask.shape[1]
    start = lax.axis_index("slab") * width
    full_index = jnp.arange(length, dtype=jnp.int32)
    part_index = start + jnp.arange(width, dtype=jnp.int32)
    full_square = frequency(full_index, length) ** 2
    part_square = frequency(part_index, length) ** 2
    total = full_square[:, None, None] + part_square[None, :, None] + full_square[None, None, :]
    unit = (2.0 * math.pi / length) ** 2
    return 4.0 * math.pi * cutoff_mask.astype(jnp.float32) / (unit * total + 0.25)


def potentials(density, fxc, cutoff_mask):
    length = density.shape[-1]
    cosine, sine = dft_tables(length)
    along_z = "abcd,de->abce"
    along_y = "abcd,ce->abed"
    along_x = "abcd,be->aecd"
    spectrum = transform(density, along_z, cosine, sine, -1.0)
    spectrum = transform(spectrum, along_y, cosine, sine, -1.0)
    kernel = column_kernel(cutoff_mask, length)
    columns = lax.all_to_all(spectrum, "slab", split_axis=3, concat_axis=2, tiled=True)
    columns = transform(columns, along_x, cosine, sine, -1.0)
    columns = columns * kernel[None, None]
    columns = transform(columns, along_x, cosine, sine, 1.0)
    result = lax.all_to_all(columns, "slab", split_axis=2, concat_axis=3, tiled=True)
    result = transform(result, along_y, cosine, sine, 1.0)
    result = transform(result, along_z, cosine, sine, 1.0)
    scale = 1.0 / float(length * length * length)
    return result * scale + fxc[None, None] * density


def per_device(drho_part, fxc, cutoff_mask, owner_table):
    local = drho_part[0]
    ordered = jnp.take(local, owner_table, axis=0)
    summed = lax.psum(ordered, "pool")
    return potentials(summed, fxc, cutoff_mask)


def solution(mesh):
    placed = (
        P("pool", "group", None, "slab", None, None),
        P("slab", None, None),
        P(None, "slab", None),
        P("group"),
    )
    return jax.shard_map(
        per_device,
        mesh=mesh,
        in_specs=placed,
        out_specs=P("group", None, "slab", None, None),
        check_vma=False,
    )
```

profile of v0, /device:TPU:0, one launch (start us, length us, event | category | flops | bytes accessed | tf_op | source)
XLA Modules:
  0.0 558.5 jit_solution(16981774304623706041)
XLA Ops:
  1.3 7.9 %gather_fusion = f32[16,2,4,128,128]{4,3,2,1,0:T(8,128)} fusion(f32[16,2,4,128,128]{4,3,2,1,0:T(8,128)} %bitcast.184, s32[1024]{0:T(1024)S(1)} %pad_clamp_fusion), kind=kCustom, calls=%fused_computation | custom fusion | bytes 16777280 | tf_op jit(solution)/shard_map/jit(_take)/gather | solution.py:65
  9.2 4.3 copy_select_fusion
  20.9 4.0 multiply_subtract_fusion
  24.9 4.1 fusion.55
  32.6 4.2 fusion.49
  36.9 4.7 subtract_bitcast_fusion.3
  41.6 4.7 add_bitcast_fusion.3
  46.3 3.8 pad_maximum_fusion
  50.1 12.2 %copy.51 = f32[16,2,4,128,128]{4,2,0,1,3:T(4,128)} copy(f32[16,2,4,128,128]{4,3,2,0,1:T(8,128)} %pad_maximum_fusion) | data formatting | bytes 16777216 | tf_op jit(solution)/shard_map/stack | solution.py:24
  62.3 7.5 %all-to-all-start = ((f32[16,2,4,128,128]{4,2,0,1,3:T(4,128)}), f32[16,2,4,128,128]{4,2,0,1,3:T(4,128)}, u32[]{:S(2)}, u32[]{:S(2)}) async-start(f32[16,2,4,128,128]{4,2,0,1,3:T(4,128)} %copy.51), calls=%async_computation | async-start | bytes 16777216 | tf_op jit(solution)/shard_map/all_to_all | solution.py:52
  70.1 185.5 %all-to-all-done = f32[16,2,4,128,128]{4,2,0,1,3:T(4,128)} async-done(((f32[16,2,4,128,128]{4,2,0,1,3:T(4,128)}), f32[16,2,4,128,128]{4,2,0,1,3:T(4,128)}, u32[]{:S(2)}, u32[]{:S(2)}) %all-to-all-start) | async-done | bytes 8388640 | tf_op jit(solution)/shard_map/all_to_all | solution.py:52
  255.6 9.1 %copy.52 = f32[16,2,4,32,4,128]{5,2,3,4,0,1:T(4,128)} copy(f32[16,2,4,32,4,128]{5,2,0,1,4,3:T(4,128)} %bitcast.20) | data formatting | bytes 16777216 | tf_op jit(solution)/shard_map/all_to_all | solution.py:52
  264.7 6.6 %fusion.14 = f32[128,16,4,128]{3,0,2,1:T(8,128)S(1)} fusion(f32[16,2,128,4,128]{4,2,3,0,1:T(8,128)} %bitcast.179), kind=kOutput, calls=%fused_computation.38 | convolution fusion | flops 1610842112 | bytes 8388608 | tf_op jit(solution)/shard_map/abcd,be->aecd/dot_general | solution.py:20
  271.3 4.0 fusion.13
  275.3 4.7 subtract_bitcast_fusion.2
  280.0 4.9 add_bitcast_fusion.2
  286.5 4.1 fusion.18
  290.6 4.1 fusion.17
  294.7 4.9 subtract_bitcast_fusion.1
  299.7 4.5 add_bitcast_fusion.1
  304.2 3.8 pad_maximum_fusion.1
  308.0 12.2 %copy.62 = f32[16,2,128,4,128]{4,3,0,1,2:T(4,128)} copy(f32[16,2,128,4,128]{4,2,3,0,1:T(8,128)} %pad_maximum_fusion.1) | data formatting | bytes 16777216 | tf_op jit(solution)/shard_map/stack | solution.py:24
  320.2 187.2 %all_to_all.36 = f32[16,2,128,4,128]{4,3,0,1,2:T(4,128)} all-to-all(f32[16,2,128,4,128]{4,3,0,1,2:T(4,128)} %copy.62), channel_id=1, replica_groups=mesh['group'=1,'pool'=1,'slab'=32] {'slab'}, dimensions={2} | all-to-all | bytes 16777216 | tf_op jit(solution)/shard_map/all_to_all | solution.py:56
  507.4 9.0 %copy.63 = f32[16,2,32,4,4,128]{5,4,2,3,0,1:T(4,128)} copy(f32[16,2,32,4,4,128]{5,4,0,1,3,2:T(4,128)} %bitcast.183) | data formatting | bytes 16777216 | tf_op jit(solution)/shard_map/all_to_all | solution.py:56
  516.4 6.1 %fusion.22 = f32[128,16,4,128]{3,0,2,1:T(8,128)S(1)} fusion(f32[16,2,4,128,128]{4,3,2,0,1:T(8,128)} %bitcast.175), kind=kOutput, calls=%fused_computation.46 | convolution fusion | flops 1610842112 | bytes 8388608 | tf_op jit(solution)/shard_map/abcd,ce->abed/dot_general | solution.py:20
  522.5 4.0 fusion.21
  526.6 4.1 fusion.26
  530.7 4.0 fusion.3
  534.7 3.8 fusion.1
  538.5 4.3 fusion.25
  546.7 4.0 add_bitcast_fusion
  553.6 4.4 copy.68
  (27 shorter events, 21.0 us)
Async XLA Ops:
  62.3 7.6 %copy-start.3 = (s32[128,4,128]{2,1,0:T(4,128)S(1)}, s32[128,4,128]{2,1,0:T(4,128)}, u32[]{:S(2)}) copy-start(s32[128,4,128]{2,1,0:T(4,128)} %param.6) | copy-start | bytes 786436
  62.3 193.4 %all-to-all-start = ((f32[16,2,4,128,128]{4,2,0,1,3:T(4,128)}), f32[16,2,4,128,128]{4,2,0,1,3:T(4,128)}, u32[]{:S(2)}, u32[]{:S(2)}) async-start(f32[16,2,4,128,128]{4,2,0,1,3:T(4,128)} %copy.51), calls=%async_computation | async-start | bytes 16777216 | tf_op jit(solution)/shard_map/all_to_all | solution.py:52
  264.7 6.6 %copy-start.1 = (f32[16,2,4,32,4,128]{5,2,3,4,0,1:T(4,128)S(1)}, f32[16,2,4,32,4,128]{5,2,3,4,0,1:T(4,128)}, u32[]{:S(2)}) copy-start(f32[16,2,4,32,4,128]{5,2,3,4,0,1:T(4,128)} %copy.52) | copy-start | bytes 25165828
  516.4 6.1 %copy-start = (f32[16,2,32,4,4,128]{5,4,2,3,0,1:T(4,128)S(1)}, f32[16,2,32,4,4,128]{5,4,2,3,0,1:T(4,128)}, u32[]{:S(2)}) copy-start(f32[16,2,32,4,4,128]{5,4,2,3,0,1:T(4,128)} %copy.63) | copy-start | bytes 25165828
  542.8 7.9 %slice-start = ((s8[8388608]{0:T(1024)(128)(4,1)}), s8[4194304]{0:T(1024)(128)(4,1)S(1)}, s32[]{:S(2)}) async-start(s8[8388608]{0:T(1024)(128)(4,1)} %bitcast.173), calls=%async_computation.2 | async-start | bytes 8388608
  546.6 4.1 slice-start.1
  546.6 4.1 copy-start.2
where the time goes:
time: 567 us; the launch traced here: 558 us
  blocking collectives  187 us (33%)
  waiting for transfers between devices  186 us (33%)
  matrix products  105 us (19%)
  local copies, waits for them, and re-layouts  54.8 us (10%)
  other arithmetic  18.1 us (3%)
  starting transfers between devices  7.45 us (1%)
    all_to_all x1, blocking collectives, potentials(): lax.all_to_all(columns, 'slab', split_axis=2, concat_axis=3, tiled=True)  187 us
    all_to_all x1, waiting for transfers between devices, potentials(): lax.all_to_all(spectrum, 'slab', split_axis=3, concat_axis=2, tiled=True)  186 us
    dot_general x6, matrix products, transform(): real_cos = jnp.einsum(form, real_part, cosine, precision=highest)  28.2 us
    dot_general x6, matrix products, transform(): imag_sin = jnp.einsum(form, imag_part, sine, precision=highest)  26.7 us
    dot_general x6, matrix products, transform(): imag_cos = jnp.einsum(form, imag_part, cosine, precision=highest)  25.1 us
    dot_general x6, matrix products, transform(): real_sin = jnp.einsum(form, real_part, sine, precision=highest)  24.5 us
    another operation x2, local copies, waits for them, and re-layouts, transform(): jnp.stack([real_cos - orient * imag_sin, imag_cos + orient * real_sin], a...  24.4 us
  transfers between devices with their start and end apart: 1, of which 1 were waited for; matrix products, arithmetic and copies ran while one was open for 0% of the time, Pallas kernels for 0%

commit v1 on v0

v1 whole, which is shorter than its diff:
```python
import functools
import math

import jax
import jax.numpy as jnp
import numpy as np
from jax import lax
from jax.experimental import pallas as pl
from jax.experimental.pallas import tpu as pltpu
from jax.sharding import PartitionSpec as P

CHUNKS = 2
VMEM_MIB = 60


def halves(matrix):
    high = matrix.astype(np.float32).astype(jnp.bfloat16)
    low = (matrix - high.astype(np.float64)).astype(np.float32).astype(jnp.bfloat16)
    return np.stack([high, low])


def complex_dft(length, sign):
    index = np.arange(length)
    angle = (index[:, None] * index[None, :] % length) * (2.0 * math.pi / length)
    cosine, sine = np.cos(angle), sign * np.sin(angle)
    return np.block([[cosine, -sine], [sine, cosine]])


def slab_order(length, width):
    table = np.arange(2 * length).reshape(2, length // width, width)
    return table.transpose(1, 0, 2).reshape(-1)


def inner_order(length, width):
    table = np.arange(2 * length).reshape(2, length // width, width)
    return table.transpose(2, 0, 1).reshape(-1)


def split(value):
    high = value.astype(jnp.bfloat16)
    low = (value - high.astype(jnp.float32)).astype(jnp.bfloat16)
    return high, low


def dot(left, right):
    return jnp.dot(left, right, preferred_element_type=jnp.float32)


def left_dot(matrix_ref, value):
    high, low = split(value)
    return dot(matrix_ref[0], high) + (dot(matrix_ref[1], high) + dot(matrix_ref[0], low))


def right_dot(value, matrix_ref):
    high, low = split(value)
    return dot(high, matrix_ref[0]) + (dot(low, matrix_ref[0]) + dot(high, matrix_ref[1]))


def forward_kernel(owner_ref, field_ref, along_z_ref, along_y_ref, out_ref):
    _, _, width, length, _ = field_ref.shape
    slabs = length // width
    rows = width * length
    field = jnp.concatenate(
        [field_ref[0, 0].reshape(rows, length), field_ref[0, 1].reshape(rows, length)], axis=1
    )
    field = right_dot(field, along_z_ref)
    field = jnp.concatenate(
        [
            jnp.concatenate(
                [field[x * length : (x + 1) * length, c * length : (c + 1) * length] for c in range(2)], axis=0
            )
            for x in range(width)
        ],
        axis=1,
    )
    field = left_dot(along_y_ref, field)
    for y in range(width):
        for c in range(2):
            first = (y * 2 + c) * slabs
            for x in range(width):
                out_ref[:, 0, c * width + x, y * length : (y + 1) * length] = field[
                    first : first + slabs, x * length : (x + 1) * length
                ]


def column_stage(field_ref, screen_ref, forth_ref, back_ref, out_ref):
    slabs, _, rows, lanes = field_ref.shape
    length = screen_ref.shape[0]
    field = field_ref[:, 0].reshape(slabs * rows, lanes)
    field = left_dot(forth_ref, field)
    screen = screen_ref[...]
    field = jnp.concatenate([field[:length] * screen, field[length:] * screen], axis=0)
    field = left_dot(back_ref, field)
    out_ref[:, 0] = field.reshape(slabs, rows, lanes)


def backward_kernel(owner_ref, field_ref, density_ref, fxc_ref, along_y_ref, along_z_ref, *rest):
    out_ref = rest[-1]
    _, _, width, length, _ = density_ref.shape
    field = jnp.concatenate(
        [
            jnp.concatenate(
                [
                    field_ref[:, 0, c * width + x, y * length : (y + 1) * length]
                    for y in range(width)
                    for c in range(2)
                ],
                axis=0,
            )
            for x in range(width)
        ],
        axis=1,
    )
    field = left_dot(along_y_ref, field)
    field = jnp.concatenate(
        [
            jnp.concatenate(
                [field[c * length : (c + 1) * length, x * length : (x + 1) * length] for c in range(2)], axis=1
            )
            for x in range(width)
        ],
        axis=0,
    )
    field = right_dot(field, along_z_ref)
    fxc = fxc_ref[...]
    for c in range(2):
        part = field[:, c * length : (c + 1) * length].reshape(width, length, length)
        out_ref[0, c] = part + fxc * density_ref[0, c]


def frequency(index, length):
    return ((index + length // 2) % length - length // 2).astype(jnp.float32)


def column_screen(cutoff_mask, length):
    width = cutoff_mask.shape[1]
    start = lax.axis_index("slab") * width
    full_index = jnp.arange(length, dtype=jnp.int32)
    part_index = start + jnp.arange(width, dtype=jnp.int32)
    full_square = frequency(full_index, length) ** 2
    part_square = frequency(part_index, length) ** 2
    total = full_square[:, None, None] + part_square[None, :, None] + full_square[None, None, :]
    unit = (2.0 * math.pi / length) ** 2
    screen = 4.0 * math.pi * cutoff_mask.astype(jnp.float32) / (unit * total + 0.25)
    return (screen * (1.0 / float(length**3))).reshape(length, width * length)


def whole_spec(array):
    zeros = (0,) * array.ndim
    return pl.BlockSpec(array.shape, lambda *_: zeros)


def cost(count, rows, length):
    size = 2 * rows * length
    return pl.CostEstimate(flops=count * 24 * size * length, bytes_accessed=count * 8 * size, transcendentals=0)


def per_device(drho_part, fxc, cutoff_mask, owner_table):
    density = drho_part[0]
    if lax.axis_size("pool") > 1:
        density = lax.psum(density, "pool")
    count, _, width, length, _ = density.shape
    slabs = length // width
    rows, lanes = 2 * width, width * length
    chunks = math.gcd(CHUNKS, count)
    each = count // chunks

    forth, back = complex_dft(length, -1.0), complex_dft(length, 1.0)
    by_slab, by_inner = slab_order(length, width), inner_order(length, width)
    z_forth, z_back = jnp.asarray(halves(forth.T)), jnp.asarray(halves(back.T))
    y_forth, y_back = jnp.asarray(halves(forth[by_inner])), jnp.asarray(halves(back[:, by_inner]))
    x_forth, x_back = jnp.asarray(halves(forth[:, by_slab])), jnp.asarray(halves(back[by_slab]))
    screen = column_screen(cutoff_mask, length)

    params = pltpu.CompilerParams(dimension_semantics=("arbitrary",), vmem_limit_bytes=VMEM_MIB * 2**20)
    packed = jax.ShapeDtypeStruct((slabs, each, rows, lanes), jnp.float32)
    packed_spec = pl.BlockSpec((slabs, 1, rows, lanes), lambda i, *_: (0, i, 0, 0))
    price = cost(each, lanes, length)

    def forward(chunk):
        return pl.pallas_call(
            forward_kernel,
            out_shape=packed,
            grid_spec=pltpu.PrefetchScalarGridSpec(
                num_scalar_prefetch=1,
                grid=(each,),
                in_specs=[
                    pl.BlockSpec(
                        (1, 2, width, length, length), lambda i, owner: (owner[chunk * each + i], 0, 0, 0, 0)
                    ),
                    whole_spec(z_forth),
                    whole_spec(y_forth),
                ],
                out_specs=packed_spec,
            ),
            compiler_params=params,
            cost_estimate=price,
        )(owner_table, density, z_forth, y_forth)

    def columns(field):
        return pl.pallas_call(
            column_stage,
            out_shape=packed,
            grid=(each,),
            in_specs=[packed_spec, whole_spec(screen), whole_spec(x_forth), whole_spec(x_back)],
            out_specs=packed_spec,
            compiler_params=params,
            cost_estimate=price,
        )(field, screen, x_forth, x_back)

    def backward(chunk, field, result):
        earlier = [] if result is None else [result]
        return pl.pallas_call(
            backward_kernel,
            out_shape=jax.ShapeDtypeStruct(density.shape, jnp.float32),
            grid_spec=pltpu.PrefetchScalarGridSpec(
                num_scalar_prefetch=1,
                grid=(each,),
                in_specs=[
                    packed_spec,
                    pl.BlockSpec(
                        (1, 2, width, length, length), lambda i, owner: (owner[chunk * each + i], 0, 0, 0, 0)
                    ),
                    whole_spec(fxc),
                    whole_spec(y_back),
                    whole_spec(z_back),
                ]
                + [pl.BlockSpec(memory_space=pl.ANY)] * len(earlier),
                out_specs=pl.BlockSpec(
                    (1, 2, width, length, length), lambda i, owner: (chunk * each + i, 0, 0, 0, 0)
                ),
            ),
            input_output_aliases={6: 0} if earlier else {},
            compiler_params=params,
            cost_estimate=price,
        )(owner_table, field, density, fxc, y_back, z_back, *earlier)

    def swap(field):
        return lax.all_to_all(field, "slab", split_axis=0, concat_axis=0, tiled=True)

    spectra = [swap(forward(chunk)) for chunk in range(chunks)]
    spectra = [swap(columns(field)) for field in spectra]
    result = None
    for chunk, field in enumerate(spectra):
        result = backward(chunk, field, result)
    return result


def solution(mesh):
    placed = (
        P("pool", "group", None, "slab", None, None),
        P("slab", None, None),
        P(None, "slab", None),
        P("group"),
    )
    return jax.shard_map(
        per_device,
        mesh=mesh,
        in_specs=placed,
        out_specs=P("group", None, "slab", None, None),
        check_vma=False,
    )
```

time: 567 us -> 421 us (0.74); the launches traced: 558 us -> 420 us
  blocking collectives: 187 us -> 0 us
  waiting for transfers between devices: 186 us -> 330 us
  matrix products: 105 us -> 0 us
  Pallas kernels: 0 us -> 68.5 us
  local copies, waits for them, and re-layouts: 54.8 us -> 0.72 us
  other arithmetic: 18.1 us -> 0.32 us
  starting transfers between devices: 7.45 us -> 20.2 us
    all_to_all x1 -> x0, blocking collectives: 187 us -> none  [potentials(): lax.all_to_all(columns, 'slab', split_axis=2, concat_axis=3, tiled=True)]
    all_to_all x1 -> x4, waiting for transfers between devices: 186 us -> 330 us  [swap(): lax.all_to_all(field, 'slab', split_axis=0, concat_axis=0, tiled=True)]
    dot_general x24 -> x0, matrix products: 105 us -> none  [the longest x6 28.2 us: transform(): real_cos = jnp.einsum(form, real_part, cosine, precision=highest)]
    pallas_call x0 -> x6, Pallas kernels: none -> 68.5 us  [the longest x2 25.4 us: forward(): pl.pallas_call(forward_kernel, out_shape=packed, grid_spec=pltpu.Prefetch...]
    another operation x2 -> x0, local copies, waits for them, and re-layouts: 24.4 us -> none  [transform(): jnp.stack([real_cos - orient * imag_sin, imag_cos + orient * real_sin], a...]
    all_to_all x2 -> x0, local copies, waits for them, and re-layouts: 18.1 us -> none  [the longest x1 9.05 us: potentials(): lax.all_to_all(spectrum, 'slab', split_axis=3, concat_axis=2, tiled=True)]
    all_to_all x1 -> x4, starting transfers between devices: 7.45 us -> 20.2 us  [swap(): lax.all_to_all(field, 'slab', split_axis=0, concat_axis=0, tiled=True)]
    gather x1 -> x0, local copies, waits for them, and re-layouts: 7.86 us -> none  [per_device(): ordered = jnp.take(local, owner_table, axis=0)]
  transfers between devices with their start and end apart: 1 -> 4, of which waited for: 1 -> 4; matrix products, arithmetic and copies ran while one was open for 0% -> 0% of each run, Pallas kernels for 0% -> 10%
where the time goes in v1:
time: 421 us; the launch traced here: 420 us
  waiting for transfers between devices  330 us (78%)
  Pallas kernels  68.5 us (16%)
  starting transfers between devices  20.2 us (5%)
    all_to_all x4, waiting for transfers between devices, swap(): lax.all_to_all(field, 'slab', split_axis=0, concat_axis=0, tiled=True)  330 us
    pallas_call x2, Pallas kernels, forward(): pl.pallas_call(forward_kernel, out_shape=packed, grid_spec=pltpu.Prefetch...  25.4 us
    pallas_call x2, Pallas kernels, backward(): pl.pallas_call(backward_kernel, out_shape=jax.ShapeDtypeStruct(density.sh...  23.7 us
    all_to_all x4, starting transfers between devices, swap(): lax.all_to_all(field, 'slab', split_axis=0, concat_axis=0, tiled=True)  20.2 us
    pallas_call x2, Pallas kernels, columns(): pl.pallas_call(column_stage, out_shape=packed, grid=(each,), in_specs=[pa...  19.4 us
  transfers between devices with their start and end apart: 4, of which 4 were waited for; matrix products, arithmetic and copies ran while one was open for 0% of the time, Pallas kernels for 10%

profile of v1, /device:TPU:0, one launch (start us, length us, event | category | flops | bytes accessed | tf_op | source)
XLA Modules:
  0.0 419.6 jit_solution(11006048990026255904)
XLA Ops:
  0.0 12.7 %shard_map.102 = f32[32,8,8,512]{3,2,1,0:T(8,128)} custom-call(s32[16]{0:T(128)} %owner_ref.7, f32[16,2,4,128,128]{4,3,2,1,0:T(8,128)} %bitcast.5, bf16[2,256,256]{2,1,0:T(8,128)(2,1)} %constant.57.clone.along_z_ref, bf16[2,256,256]{2,1,0:T(8,128)(2,1)} %constant.59.clone.along_y_ref), custom_call_target="tpu_custom_call" | custom-call | flops 3221225472 | bytes 8388608 | tf_op jit(solution)/shard_map/pallas_call | solution.py:181
  12.7 7.5 %all-to-all-start.2 = ((f32[32,8,8,512]{3,2,1,0:T(8,128)}), f32[32,8,8,512]{3,2,1,0:T(8,128)}, u32[]{:S(2)}, u32[]{:S(2)}) async-start(f32[32,8,8,512]{3,2,1,0:T(8,128)} %shard_map.102), calls=%async_computation.2 | async-start | bytes 8388608 | tf_op jit(solution)/shard_map/all_to_all | solution.py:239
  20.2 12.7 %shard_map.100 = f32[32,8,8,512]{3,2,1,0:T(8,128)} custom-call(s32[16]{0:T(128)} %owner_ref.7, f32[16,2,4,128,128]{4,3,2,1,0:T(8,128)} %bitcast.6, bf16[2,256,256]{2,1,0:T(8,128)(2,1)} %constant.57.clone.along_z_ref, bf16[2,256,256]{2,1,0:T(8,128)(2,1)} %constant.59.clone.along_y_ref), custom_call_target="tpu_custom_call" | custom-call | flops 3221225472 | bytes 8388608 | tf_op jit(solution)/shard_map/pallas_call | solution.py:181
  32.8 0.0 copy-start
  32.8 81.0 %all-to-all-done.2.field_ref = f32[32,8,8,512]{3,2,1,0:T(8,128)} async-done(((f32[32,8,8,512]{3,2,1,0:T(8,128)}), f32[32,8,8,512]{3,2,1,0:T(8,128)}, u32[]{:S(2)}, u32[]{:S(2)}) %all-to-all-start.2) | async-done | bytes 4194336 | tf_op jit(solution)/shard_map/all_to_all | solution.py:239
  113.9 4.2 %all-to-all-start = ((f32[32,8,8,512]{3,2,1,0:T(8,128)}), f32[32,8,8,512]{3,2,1,0:T(8,128)}, u32[]{:S(2)}, u32[]{:S(2)}) async-start(f32[32,8,8,512]{3,2,1,0:T(8,128)} %shard_map.100), calls=%async_computation | async-start | bytes 8388608 | tf_op jit(solution)/shard_map/all_to_all | solution.py:239
  118.2 0.1 broadcast_add_fusion
  118.2 0.0 copy-done
  118.3 0.2 fusion
  118.5 0.7 copy.14
  119.2 9.7 %shard_map.103 = f32[32,8,8,512]{3,2,1,0:T(8,128)} custom-call(f32[32,8,8,512]{3,2,1,0:T(8,128)} %all-to-all-done.2.field_ref, f32[128,512]{1,0:T(8,128)} %bitcast.10, bf16[2,256,256]{2,1,0:T(8,128)(2,1)} %constant.61.clone.forth_ref, bf16[2,256,256]{2,1,0:T(8,128)(2,1)} %constant.62.clone.back_ref), custom_call_target="tpu_custom_call" | custom-call | flops 3221225472 | bytes 8388608 | tf_op jit(solution)/shard_map/pallas_call | solution.py:201
  128.9 82.9 %all-to-all-done.field_ref = f32[32,8,8,512]{3,2,1,0:T(8,128)} async-done(((f32[32,8,8,512]{3,2,1,0:T(8,128)}), f32[32,8,8,512]{3,2,1,0:T(8,128)}, u32[]{:S(2)}, u32[]{:S(2)}) %all-to-all-start) | async-done | bytes 4194336 | tf_op jit(solution)/shard_map/all_to_all | solution.py:239
  211.8 4.2 %all-to-all-start.3 = ((f32[32,8,8,512]{3,2,1,0:T(8,128)}), f32[32,8,8,512]{3,2,1,0:T(8,128)}, u32[]{:S(2)}, u32[]{:S(2)}) async-start(f32[32,8,8,512]{3,2,1,0:T(8,128)} %shard_map.103), calls=%async_computation.3 | async-start | bytes 8388608 | tf_op jit(solution)/shard_map/all_to_all | solution.py:239
  216.1 9.7 %shard_map.101 = f32[32,8,8,512]{3,2,1,0:T(8,128)} custom-call(f32[32,8,8,512]{3,2,1,0:T(8,128)} %all-to-all-done.field_ref, f32[128,512]{1,0:T(8,128)} %bitcast.11, bf16[2,256,256]{2,1,0:T(8,128)(2,1)} %constant.61.clone.forth_ref, bf16[2,256,256]{2,1,0:T(8,128)(2,1)} %constant.62.clone.back_ref), custom_call_target="tpu_custom_call" | custom-call | flops 3221225472 | bytes 8388608 | tf_op jit(solution)/shard_map/pallas_call | solution.py:201
  225.8 84.0 %all-to-all-done.3.field_ref = f32[32,8,8,512]{3,2,1,0:T(8,128)} async-done(((f32[32,8,8,512]{3,2,1,0:T(8,128)}), f32[32,8,8,512]{3,2,1,0:T(8,128)}, u32[]{:S(2)}, u32[]{:S(2)}) %all-to-all-start.3) | async-done | bytes 4194336 | tf_op jit(solution)/shard_map/all_to_all | solution.py:239
  309.8 4.2 %all-to-all-start.1 = ((f32[32,8,8,512]{3,2,1,0:T(8,128)}), f32[32,8,8,512]{3,2,1,0:T(8,128)}, u32[]{:S(2)}, u32[]{:S(2)}) async-start(f32[32,8,8,512]{3,2,1,0:T(8,128)} %shard_map.101), calls=%async_computation.1 | async-start | bytes 8388608 | tf_op jit(solution)/shard_map/all_to_all | solution.py:239
  314.0 11.8 %shard_map.104.rest_0_ = f32[16,2,4,128,128]{4,3,2,1,0:T(8,128)} custom-call(s32[16]{0:T(128)} %owner_ref.7, f32[32,8,8,512]{3,2,1,0:T(8,128)} %all-to-all-done.3.field_ref, f32[16,2,4,128,128]{4,3,2,1,0:T(8,128)} %bitcast.7, f32[4,128,128]{2,1,0:T(8,128)} %fxc_ref.3, bf16[2,256,256]{2,1,0:T(8,128)(2,1)} %constant.60.clone.along_y_ref, ...), custom_call_target="tpu_custom_call" | custom-call | flops 3221225472 | bytes 8388608 | tf_op jit(solution)/shard_map/pallas_call | solution.py:213
  325.9 81.9 %all-to-all-done.1.field_ref = f32[32,8,8,512]{3,2,1,0:T(8,128)} async-done(((f32[32,8,8,512]{3,2,1,0:T(8,128)}), f32[32,8,8,512]{3,2,1,0:T(8,128)}, u32[]{:S(2)}, u32[]{:S(2)}) %all-to-all-start.1) | async-done | bytes 4194336 | tf_op jit(solution)/shard_map/all_to_all | solution.py:239
  407.7 11.8 %shard_map.105 = f32[16,2,4,128,128]{4,3,2,1,0:T(8,128)} custom-call(s32[16]{0:T(128)} %owner_ref.7, f32[32,8,8,512]{3,2,1,0:T(8,128)} %all-to-all-done.1.field_ref, f32[16,2,4,128,128]{4,3,2,1,0:T(8,128)} %bitcast.8, f32[4,128,128]{2,1,0:T(8,128)} %fxc_ref.3, bf16[2,256,256]{2,1,0:T(8,128)(2,1)} %constant.60.clone.along_y_ref, ...), custom_call_target="tpu_custom_call", output_to_operand_aliasing={{}: (6, {})} | custom-call | flops 3221225472 | bytes 8388608 | tf_op jit(solution)/shard_map/pallas_call | solution.py:213
  (2 shorter events, 0.0 us)
Async XLA Ops:
  12.7 101.2 %all-to-all-start.2 = ((f32[32,8,8,512]{3,2,1,0:T(8,128)}), f32[32,8,8,512]{3,2,1,0:T(8,128)}, u32[]{:S(2)}, u32[]{:S(2)}) async-start(f32[32,8,8,512]{3,2,1,0:T(8,128)} %shard_map.102), calls=%async_computation.2 | async-start | bytes 8388608 | tf_op jit(solution)/shard_map/all_to_all | solution.py:239
  32.8 85.4 %copy-start = (s32[128,4,128]{2,1,0:T(4,128)S(1)}, s32[128,4,128]{2,1,0:T(4,128)}, u32[]{:S(2)}) copy-start(s32[128,4,128]{2,1,0:T(4,128)} %param.12) | copy-start | bytes 786436
  113.9 97.9 %all-to-all-start = ((f32[32,8,8,512]{3,2,1,0:T(8,128)}), f32[32,8,8,512]{3,2,1,0:T(8,128)}, u32[]{:S(2)}, u32[]{:S(2)}) async-start(f32[32,8,8,512]{3,2,1,0:T(8,128)} %shard_map.100), calls=%async_computation | async-start | bytes 8388608 | tf_op jit(solution)/shard_map/all_to_all | solution.py:239
  211.8 97.9 %all-to-all-start.3 = ((f32[32,8,8,512]{3,2,1,0:T(8,128)}), f32[32,8,8,512]{3,2,1,0:T(8,128)}, u32[]{:S(2)}, u32[]{:S(2)}) async-start(f32[32,8,8,512]{3,2,1,0:T(8,128)} %shard_map.103), calls=%async_computation.3 | async-start | bytes 8388608 | tf_op jit(solution)/shard_map/all_to_all | solution.py:239
  309.8 97.9 %all-to-all-start.1 = ((f32[32,8,8,512]{3,2,1,0:T(8,128)}), f32[32,8,8,512]{3,2,1,0:T(8,128)}, u32[]{:S(2)}, u32[]{:S(2)}) async-start(f32[32,8,8,512]{3,2,1,0:T(8,128)} %shard_map.101), calls=%async_computation.1 | async-start | bytes 8388608 | tf_op jit(solution)/shard_map/all_to_all | solution.py:239

commit v2 on v1

--- a/solution.py
+++ b/solution.py
@@ -11,6 +11,7 @@
 
 CHUNKS = 2
 VMEM_MIB = 60
+PER_STEP = 2
 
 
 def halves(matrix):
@@ -56,76 +57,91 @@
     return dot(high, matrix_ref[0]) + (dot(low, matrix_ref[0]) + dot(high, matrix_ref[1]))
 
 
-def forward_kernel(owner_ref, field_ref, along_z_ref, along_y_ref, out_ref):
-    _, _, width, length, _ = field_ref.shape
+def forward_kernel(owner_ref, *refs):
+    *field_refs, along_z_ref, along_y_ref, out_ref = refs
+    _, _, width, length, _ = field_refs[0].shape
     slabs = length // width
     rows = width * length
-    field = jnp.concatenate(
-        [field_ref[0, 0].reshape(rows, length), field_ref[0, 1].reshape(rows, length)], axis=1
-    )
-    field = right_dot(field, along_z_ref)
-    field = jnp.concatenate(
-        [
-            jnp.concatenate(
-                [field[x * length : (x + 1) * length, c * length : (c + 1) * length] for c in range(2)], axis=0
-            )
-            for x in range(width)
-        ],
-        axis=1,
-    )
-    field = left_dot(along_y_ref, field)
-    for y in range(width):
+    fields = [
+        jnp.concatenate([ref[0, 0].reshape(rows, length), ref[0, 1].reshape(rows, length)], axis=1)
+        for ref in field_refs
+    ]
+    fields = [right_dot(field, along_z_ref) for field in fields]
+    fields = [
+        jnp.concatenate(
+            [
+                jnp.concatenate(
+                    [field[x * length : (x + 1) * length, c * length : (c + 1) * length] for c in range(2)], axis=0
+                )
+                for x in range(width)
+            ],
+            axis=1,
+        )
+        for field in fields
+    ]
+    fields = [left_dot(along_y_ref, field) for field in fields]
+    for slot, field in enumerate(fields):
+        for y in range(width):
+            for c in range(2):
+                first = (y * 2 + c) * slabs
+                for x in range(width):
+                    out_ref[:, slot, c * width + x, y * length : (y + 1) * length] = field[
+                        first : first + slabs, x * length : (x + 1) * length
+                    ]
+
+
+def column_stage(field_ref, screen_ref, forth_ref, back_ref, out_ref):
+    slabs, slots, rows, lanes = field_ref.shape
+    length = screen_ref.shape[0]
+    fields = [field_ref[:, slot].reshape(slabs * rows, lanes) for slot in range(slots)]
+    fields = [left_dot(forth_ref, field) for field in fields]
+    screen = screen_ref[...]
+    fields = [jnp.concatenate([field[:length] * screen, field[length:] * screen], axis=0) for field in fields]
+    fields = [left_dot(back_ref, field) for field in fields]
+    for slot, field in enumerate(fields):
+        out_ref[:, slot] = field.reshape(slabs, rows, lanes)
+
+
+def backward_kernel(slots, owner_ref, field_ref, *refs):
+    density_refs, out_ref = refs[:slots], refs[-1]
+    fxc_ref, along_y_ref, along_z_ref = refs[slots : slots + 3]
+    _, _, width, length, _ = density_refs[0].shape
+    fields = [
+        jnp.concatenate(
+            [
+                jnp.concatenate(
+                    [
+                        field_ref[:, slot, c * width + x, y * length : (y + 1) * length]
+                        for y in range(width)
+                        for c in range(2)
+                    ],
+                    axis=0,
+                )
+                for x in range(width)
+            ],
+            axis=1,
+        )
+        for slot in range(slots)
+    ]
+    fields = [left_dot(along_y_ref, field) for field in fields]
+    fields = [
+        jnp.concatenate(
+            [
+                jnp.concatenate(
+                    [field[c * length : (c + 1) * length, x * length : (x + 1) * length] for c in range(2)], axis=1
+                )
+                for x in range(width)
+            ],
+            axis=0,
+        )
+        for field in fields
+    ]
+    fields = [right_dot(field, along_z_ref) for field in fields]
+    fxc = fxc_ref[...]
+    for slot, field in enumerate(fields):
         for c in range(2):
-            first = (y * 2 + c) * slabs
-            for x in range(width):
-                out_ref[:, 0, c * width + x, y * length : (y + 1) * length] = field[
-                    first : first + slabs, x * length : (x + 1) * length
-                ]
-
-
-def column_stage(field_ref, screen_ref, forth_ref, back_ref, out_ref):
-    slabs, _, rows, lanes = field_ref.shape
-    length = screen_ref.shape[0]
-    field = field_ref[:, 0].reshape(slabs * rows, lanes)
-    field = left_dot(forth_ref, field)
-    screen = screen_ref[...]
-    field = jnp.concatenate([field[:length] * screen, field[length:] * screen], axis=0)
-    field = left_dot(back_ref, field)
-    out_ref[:, 0] = field.reshape(slabs, rows, lanes)
-
-
-def backward_kernel(owner_ref, field_ref, density_ref, fxc_ref, along_y_ref, along_z_ref, *rest):
-    out_ref = rest[-1]
-    _, _, width, length, _ = density_ref.shape
-    field = jnp.concatenate(
-        [
-            jnp.concatenate(
-                [
-                    field_ref[:, 0, c * width + x, y * length : (y + 1) * length]
-                    for y in range(width)
-                    for c in range(2)
-                ],
-                axis=0,
-            )
-            for x in range(width)
-        ],
-        axis=1,
-    )
-    field = left_dot(along_y_ref, field)
-    field = jnp.concatenate(
-        [
-            jnp.concatenate(
-                [field[c * length : (c + 1) * length, x * length : (x + 1) * length] for c in range(2)], axis=1
-            )
-            for x in range(width)
-        ],
-        axis=0,
-    )
-    field = right_dot(field, along_z_ref)
-    fxc = fxc_ref[...]
-    for c in range(2):
-        part = field[:, c * length : (c + 1) * length].reshape(width, length, length)
-        out_ref[0, c] = part + fxc * density_ref[0, c]
+            part = field[:, c * length : (c + 1) * length].reshape(width, length, length)
+            out_ref[slot, c] = part + fxc * density_refs[slot][0, c]
 
 
 def frequency(index, length):
@@ -164,6 +180,8 @@
     rows, lanes = 2 * width, width * length
     chunks = math.gcd(CHUNKS, count)
     each = count // chunks
+    slots = math.gcd(PER_STEP, each)
+    steps = each // slots
 
     forth, back = complex_dft(length, -1.0), complex_dft(length, 1.0)
     by_slab, by_inner = slab_order(length, width), inner_order(length, width)
@@ -174,8 +192,13 @@
 
     params = pltpu.CompilerParams(dimension_semantics=("arbitrary",), vmem_limit_bytes=VMEM_MIB * 2**20)
     packed = jax.ShapeDtypeStruct((slabs, each, rows, lanes), jnp.float32)
-    packed_spec = pl.BlockSpec((slabs, 1, rows, lanes), lambda i, *_: (0, i, 0, 0))
+    packed_spec = pl.BlockSpec((slabs, slots, rows, lanes), lambda i, *_: (0, i, 0, 0))
     price = cost(each, lanes, length)
+
+    def owned(chunk, slot):
+        return pl.BlockSpec(
+            (1, 2, width, length, length), lambda i, owner: (owner[chunk * each + i * slots + slot], 0, 0, 0, 0)
+        )
 
     def forward(chunk):
         return pl.pallas_call(
@@ -183,11 +206,9 @@
             out_shape=packed,
             grid_spec=pltpu.PrefetchScalarGridSpec(
                 num_scalar_prefetch=1,
-                grid=(each,),
-                in_specs=[
-                    pl.BlockSpec(
-                        (1, 2, width, length, length), lambda i, owner: (owner[chunk * each + i], 0, 0, 0, 0)
-                    ),
+                grid=(steps,),
+                in_specs=[owned(chunk, slot) for slot in range(slots)]
+                + [
                     whole_spec(z_forth),
                     whole_spec(y_forth),
                 ],
@@ -195,13 +216,13 @@
             ),
             compiler_params=params,
             cost_estimate=price,
-        )(owner_table, density, z_forth, y_forth)
+        )(owner_table, *[density] * slots, z_forth, y_forth)
 
     def columns(field):
         return pl.pallas_call(
             column_stage,
             out_shape=packed,
-            grid=(each,),
+            grid=(steps,),
             in_specs=[packed_spec, whole_spec(screen), whole_spec(x_forth), whole_spec(x_back)],
             out_specs=packed_spec,
             compiler_params=params,
@@ -211,29 +232,27 @@
     def backward(chunk, field, result):
         earlier = [] if result is None else [result]
         return pl.pallas_call(
-            backward_kernel,
+            functools.partial(backward_kernel, slots),
             out_shape=jax.ShapeDtypeStruct(density.shape, jnp.float32),
             grid_spec=pltpu.PrefetchScalarGridSpec(
                 num_scalar_prefetch=1,
-                grid=(each,),
-                in_specs=[
-                    packed_spec,
-                    pl.BlockSpec(
-                        (1, 2, width, length, length), lambda i, owner: (owner[chunk * each + i], 0, 0, 0, 0)
-                    ),
+                grid=(steps,),
+                in_specs=[packed_spec]
+                + [owned(chunk, slot) for slot in range(slots)]
+                + [
                     whole_spec(fxc),
                     whole_spec(y_back),
                     whole_spec(z_back),
                 ]
                 + [pl.BlockSpec(memory_space=pl.ANY)] * len(earlier),
                 out_specs=pl.BlockSpec(
-                    (1, 2, width, length, length), lambda i, owner: (chunk * each + i, 0, 0, 0, 0)
+                    (slots, 2, width, length, length), lambda i, owner: (chunk * steps + i, 0, 0, 0, 0)
                 ),
             ),
-            input_output_aliases={6: 0} if earlier else {},
+            input_output_aliases={5 + slots: 0} if earlier else {},
             compiler_params=params,
             cost_estimate=price,
-        )(owner_table, field, density, fxc, y_back, z_back, *earlier)
+        )(owner_table, field, *[density] * slots, fxc, y_back, z_back, *earlier)
 
     def swap(field):
         return lax.all_to_all(field, "slab", split_axis=0, concat_axis=0, tiled=True)

time: 421 us -> 415 us (0.986)
  Pallas kernels: 68.5 us -> 51.7 us
  waiting for transfers between devices: 330 us -> 341 us
    all_to_all x4, waiting for transfers between devices: 330 us -> 341 us  [swap(): lax.all_to_all(field, 'slab', split_axis=0, concat_axis=0, tiled=True)]
    pallas_call x4, Pallas kernels: 43.1 us -> 33.6 us  [the longest x2 19.1 us: backward(): pl.pallas_call(functools.partial(backward_kernel, slots), out_shape=jax.S...]
    pallas_call x2, Pallas kernels: 25.4 us -> 18.1 us  [forward(): pl.pallas_call(forward_kernel, out_shape=packed, grid_spec=pltpu.Prefetch...]
  transfers between devices with their start and end apart: 4 -> 4, of which waited for: 4 -> 4; matrix products, arithmetic and copies ran while one was open for 0% -> 0% of each run, Pallas kernels for 10% -> 8%
where the time goes in v2:
time: 415 us; the launch traced here: 414 us
  waiting for transfers between devices  341 us (82%)
  Pallas kernels  51.7 us (12%)
  starting transfers between devices  20.2 us (5%)
    all_to_all x4, waiting for transfers between devices, swap(): lax.all_to_all(field, 'slab', split_axis=0, concat_axis=0, tiled=True)  341 us
    all_to_all x4, starting transfers between devices, swap(): lax.all_to_all(field, 'slab', split_axis=0, concat_axis=0, tiled=True)  20.2 us
    pallas_call x2, Pallas kernels, backward(): pl.pallas_call(functools.partial(backward_kernel, slots), out_shape=jax.S...  19.1 us
    pallas_call x2, Pallas kernels, forward(): pl.pallas_call(forward_kernel, out_shape=packed, grid_spec=pltpu.Prefetch...  18.1 us
    pallas_call x2, Pallas kernels, columns(): pl.pallas_call(column_stage, out_shape=packed, grid=(steps,), in_specs=[p...  14.5 us
  transfers between devices with their start and end apart: 4, of which 4 were waited for; matrix products, arithmetic and copies ran while one was open for 0% of the time, Pallas kernels for 8%

profile of v2, /device:TPU:0, one launch (start us, length us, event | category | flops | bytes accessed | tf_op | source)
XLA Modules:
  0.0 413.6 jit_solution(17383635639696737975)
XLA Ops:
  0.0 9.1 %shard_map.102 = f32[32,8,8,512]{3,2,1,0:T(8,128)} custom-call(s32[16]{0:T(128)} %owner_ref.7, f32[16,2,4,128,128]{4,3,2,1,0:T(8,128)} %bitcast.5, f32[16,2,4,128,128]{4,3,2,1,0:T(8,128)} %bitcast.6, bf16[2,256,256]{2,1,0:T(8,128)(2,1)} %constant.57.clone.refs_2_, bf16[2,256,256]{2,1,0:T(8,128)(2,1)} %constant.59.clone.refs_3_), custom_call_target="tpu_custom_call" | custom-call | flops 3221225472 | bytes 8388608 | tf_op jit(solution)/shard_map/pallas_call | solution.py:204
  9.1 7.5 %all-to-all-start.2 = ((f32[32,8,8,512]{3,2,1,0:T(8,128)}), f32[32,8,8,512]{3,2,1,0:T(8,128)}, u32[]{:S(2)}, u32[]{:S(2)}) async-start(f32[32,8,8,512]{3,2,1,0:T(8,128)} %shard_map.102), calls=%async_computation.2 | async-start | bytes 8388608 | tf_op jit(solution)/shard_map/all_to_all | solution.py:258
  16.5 9.0 %shard_map.100 = f32[32,8,8,512]{3,2,1,0:T(8,128)} custom-call(s32[16]{0:T(128)} %owner_ref.7, f32[16,2,4,128,128]{4,3,2,1,0:T(8,128)} %bitcast.7, f32[16,2,4,128,128]{4,3,2,1,0:T(8,128)} %bitcast.8, bf16[2,256,256]{2,1,0:T(8,128)(2,1)} %constant.57.clone.refs_2_, bf16[2,256,256]{2,1,0:T(8,128)(2,1)} %constant.59.clone.refs_3_), custom_call_target="tpu_custom_call" | custom-call | flops 3221225472 | bytes 8388608 | tf_op jit(solution)/shard_map/pallas_call | solution.py:204
  25.5 0.0 copy-start
  25.5 84.7 %all-to-all-done.2.field_ref = f32[32,8,8,512]{3,2,1,0:T(8,128)} async-done(((f32[32,8,8,512]{3,2,1,0:T(8,128)}), f32[32,8,8,512]{3,2,1,0:T(8,128)}, u32[]{:S(2)}, u32[]{:S(2)}) %all-to-all-start.2) | async-done | bytes 4194336 | tf_op jit(solution)/shard_map/all_to_all | solution.py:258
  110.2 4.2 %all-to-all-start = ((f32[32,8,8,512]{3,2,1,0:T(8,128)}), f32[32,8,8,512]{3,2,1,0:T(8,128)}, u32[]{:S(2)}, u32[]{:S(2)}) async-start(f32[32,8,8,512]{3,2,1,0:T(8,128)} %shard_map.100), calls=%async_computation | async-start | bytes 8388608 | tf_op jit(solution)/shard_map/all_to_all | solution.py:258
  114.5 0.1 broadcast_add_fusion
  114.6 0.0 copy-done
  114.6 0.2 fusion
  114.8 0.7 copy.14
  115.5 7.3 %shard_map.103 = f32[32,8,8,512]{3,2,1,0:T(8,128)} custom-call(f32[32,8,8,512]{3,2,1,0:T(8,128)} %all-to-all-done.2.field_ref, f32[128,512]{1,0:T(8,128)} %bitcast.14, bf16[2,256,256]{2,1,0:T(8,128)(2,1)} %constant.61.clone.forth_ref, bf16[2,256,256]{2,1,0:T(8,128)(2,1)} %constant.62.clone.back_ref), custom_call_target="tpu_custom_call" | custom-call | flops 3221225472 | bytes 8388608 | tf_op jit(solution)/shard_map/pallas_call | solution.py:222
  122.8 85.4 %all-to-all-done.field_ref = f32[32,8,8,512]{3,2,1,0:T(8,128)} async-done(((f32[32,8,8,512]{3,2,1,0:T(8,128)}), f32[32,8,8,512]{3,2,1,0:T(8,128)}, u32[]{:S(2)}, u32[]{:S(2)}) %all-to-all-start) | async-done | bytes 4194336 | tf_op jit(solution)/shard_map/all_to_all | solution.py:258
  208.2 4.2 %all-to-all-start.3 = ((f32[32,8,8,512]{3,2,1,0:T(8,128)}), f32[32,8,8,512]{3,2,1,0:T(8,128)}, u32[]{:S(2)}, u32[]{:S(2)}) async-start(f32[32,8,8,512]{3,2,1,0:T(8,128)} %shard_map.103), calls=%async_computation.3 | async-start | bytes 8388608 | tf_op jit(solution)/shard_map/all_to_all | solution.py:258
  212.4 7.3 %shard_map.101 = f32[32,8,8,512]{3,2,1,0:T(8,128)} custom-call(f32[32,8,8,512]{3,2,1,0:T(8,128)} %all-to-all-done.field_ref, f32[128,512]{1,0:T(8,128)} %bitcast.15, bf16[2,256,256]{2,1,0:T(8,128)(2,1)} %constant.61.clone.forth_ref, bf16[2,256,256]{2,1,0:T(8,128)(2,1)} %constant.62.clone.back_ref), custom_call_target="tpu_custom_call" | custom-call | flops 3221225472 | bytes 8388608 | tf_op jit(solution)/shard_map/pallas_call | solution.py:222
  219.7 86.4 %all-to-all-done.3.field_ref = f32[32,8,8,512]{3,2,1,0:T(8,128)} async-done(((f32[32,8,8,512]{3,2,1,0:T(8,128)}), f32[32,8,8,512]{3,2,1,0:T(8,128)}, u32[]{:S(2)}, u32[]{:S(2)}) %all-to-all-start.3) | async-done | bytes 4194336 | tf_op jit(solution)/shard_map/all_to_all | solution.py:258
  306.1 4.2 %all-to-all-start.1 = ((f32[32,8,8,512]{3,2,1,0:T(8,128)}), f32[32,8,8,512]{3,2,1,0:T(8,128)}, u32[]{:S(2)}, u32[]{:S(2)}) async-start(f32[32,8,8,512]{3,2,1,0:T(8,128)} %shard_map.101), calls=%async_computation.1 | async-start | bytes 8388608 | tf_op jit(solution)/shard_map/all_to_all | solution.py:258
  310.4 9.6 %shard_map.104.refs_5_ = f32[16,2,4,128,128]{4,3,2,1,0:T(8,128)} custom-call(s32[16]{0:T(128)} %owner_ref.7, f32[32,8,8,512]{3,2,1,0:T(8,128)} %all-to-all-done.3.field_ref, f32[16,2,4,128,128]{4,3,2,1,0:T(8,128)} %bitcast.9, f32[16,2,4,128,128]{4,3,2,1,0:T(8,128)} %bitcast.10, f32[4,128,128]{2,1,0:T(8,128)} %refs_2_.5, ...), custom_call_target="tpu_custom_call" | custom-call | flops 3221225472 | bytes 8388608 | tf_op jit(solution)/shard_map/pallas_call | solution.py:234
  319.9 84.1 %all-to-all-done.1.field_ref = f32[32,8,8,512]{3,2,1,0:T(8,128)} async-done(((f32[32,8,8,512]{3,2,1,0:T(8,128)}), f32[32,8,8,512]{3,2,1,0:T(8,128)}, u32[]{:S(2)}, u32[]{:S(2)}) %all-to-all-start.1) | async-done | bytes 4194336 | tf_op jit(solution)/shard_map/all_to_all | solution.py:258
  404.1 9.6 %shard_map.105 = f32[16,2,4,128,128]{4,3,2,1,0:T(8,128)} custom-call(s32[16]{0:T(128)} %owner_ref.7, f32[32,8,8,512]{3,2,1,0:T(8,128)} %all-to-all-done.1.field_ref, f32[16,2,4,128,128]{4,3,2,1,0:T(8,128)} %bitcast.11, f32[16,2,4,128,128]{4,3,2,1,0:T(8,128)} %bitcast.12, f32[4,128,128]{2,1,0:T(8,128)} %refs_2_.5, ...), custom_call_target="tpu_custom_call", output_to_operand_aliasing={{}: (7, {})} | custom-call | flops 3221225472 | bytes 8388608 | tf_op jit(solution)/shard_map/pallas_call | solution.py:234
  (2 shorter events, 0.0 us)
Async XLA Ops:
  9.1 101.2 %all-to-all-start.2 = ((f32[32,8,8,512]{3,2,1,0:T(8,128)}), f32[32,8,8,512]{3,2,1,0:T(8,128)}, u32[]{:S(2)}, u32[]{:S(2)}) async-start(f32[32,8,8,512]{3,2,1,0:T(8,128)} %shard_map.102), calls=%async_computation.2 | async-start | bytes 8388608 | tf_op jit(solution)/shard_map/all_to_all | solution.py:258
  25.5 89.1 %copy-start = (s32[128,4,128]{2,1,0:T(4,128)S(1)}, s32[128,4,128]{2,1,0:T(4,128)}, u32[]{:S(2)}) copy-start(s32[128,4,128]{2,1,0:T(4,128)} %param.12) | copy-start | bytes 786436
  110.2 97.9 %all-to-all-start = ((f32[32,8,8,512]{3,2,1,0:T(8,128)}), f32[32,8,8,512]{3,2,1,0:T(8,128)}, u32[]{:S(2)}, u32[]{:S(2)}) async-start(f32[32,8,8,512]{3,2,1,0:T(8,128)} %shard_map.100), calls=%async_computation | async-start | bytes 8388608 | tf_op jit(solution)/shard_map/all_to_all | solution.py:258
  208.2 97.9 %all-to-all-start.3 = ((f32[32,8,8,512]{3,2,1,0:T(8,128)}), f32[32,8,8,512]{3,2,1,0:T(8,128)}, u32[]{:S(2)}, u32[]{:S(2)}) async-start(f32[32,8,8,512]{3,2,1,0:T(8,128)} %shard_map.103), calls=%async_computation.3 | async-start | bytes 8388608 | tf_op jit(solution)/shard_map/all_to_all | solution.py:258
  306.1 97.9 %all-to-all-start.1 = ((f32[32,8,8,512]{3,2,1,0:T(8,128)}), f32[32,8,8,512]{3,2,1,0:T(8,128)}, u32[]{:S(2)}, u32[]{:S(2)}) async-start(f32[32,8,8,512]{3,2,1,0:T(8,128)} %shard_map.101), calls=%async_computation.1 | async-start | bytes 8388608 | tf_op jit(solution)/shard_map/all_to_all | solution.py:258
